TPU v7x, 32 devices: a whole 2x2x4 slice. The times are simulated.
32 devices in a mesh: dp: 8 (over y, x, core), tensor: 4 (over z).
Axes of the slice: x: 2, y: 2, z: 4, core: 2. Of those that a mesh axis runs over, the one named last changes fastest.
Arguments:
- layer_input: bfloat16 [12288, 2048], P('dp'), may hold values from -30 to 30
- cotangent: bfloat16 [12288, 2048], P('dp'), may hold values from -6 to 6
- lengths: int32 [24], P('dp'), may hold values from 0 to 512, as said below
- projector: float32 [2048, 6144], P('dp', 'tensor'), may hold values from -0.125 to 0.125
- projector_moments: float32 [2, 2048, 6144], P(None, 'dp', 'tensor'), as said below
- shifts: float32 [8, 768], P('tensor', 'dp'), may hold values from -3 to 3
- shifts_moments: float32 [2, 8, 768], P(None, 'tensor', 'dp'), as said below
- combiner: float32 [2048, 2048], P('tensor', 'dp'), may hold values from -1.5 to 1.5
- combiner_moments: float32 [2, 2048, 2048], P(None, 'tensor', 'dp'), as said below
- expander: float32 [2048, 8192], P('dp', 'tensor'), may hold values from -0.125 to 0.125
- expander_moments: float32 [2, 2048, 8192], P(None, 'dp', 'tensor'), as said below
- offsets: float32 [8, 1024], P('tensor', 'dp'), may hold values from -3 to 3
- offsets_moments: float32 [2, 8, 1024], P(None, 'tensor', 'dp'), as said below
- reducer: float32 [8192, 2048], P('tensor', 'dp'), may hold values from -0.0625 to 0.0625
- reducer_moments: float32 [2, 8192, 2048], P(None, 'tensor', 'dp'), as said below
- vectors: float32 [6, 2048], P(None, ('dp', 'tensor')), may hold values from -2 to 2
- vectors_moments: float32 [2, 6, 2048], P(None, None, ('dp', 'tensor')), as said below
Outputs:
- layer_output: bfloat16 [12288, 2048], P('dp', 'tensor')
- input_gradient: bfloat16 [12288, 2048], P('dp', 'tensor')
- projector_gradient: float32 [2048, 6144], P('dp', 'tensor')
- projector_states: float32 [2, 2048, 6144], P(None, 'dp', 'tensor')
- projector_update: float32 [2048, 6144], P('dp', 'tensor')
- shifts_gradient: float32 [8, 768], P('tensor', 'dp')
- shifts_states: float32 [2, 8, 768], P(None, 'tensor', 'dp')
- shifts_update: float32 [8, 768], P('tensor', 'dp')
- combiner_gradient: float32 [2048, 2048], P('tensor', 'dp')
- combiner_states: float32 [2, 2048, 2048], P(None, 'tensor', 'dp')
- combiner_update: float32 [2048, 2048], P('tensor', 'dp')
- expander_gradient: float32 [2048, 8192], P('dp', 'tensor')
- expander_states: float32 [2, 2048, 8192], P(None, 'dp', 'tensor')
- expander_update: float32 [2048, 8192], P('dp', 'tensor')
- offsets_gradient: float32 [8, 1024], P('tensor', 'dp')
- offsets_states: float32 [2, 8, 1024], P(None, 'tensor', 'dp')
- offsets_update: float32 [8, 1024], P('tensor', 'dp')
- reducer_gradient: float32 [8192, 2048], P('tensor', 'dp')
- reducer_states: float32 [2, 8192, 2048], P(None, 'tensor', 'dp')
- reducer_update: float32 [8192, 2048], P('tensor', 'dp')
- vectors_gradient: float32 [6, 2048], P(None, ('dp', 'tensor'))
- vectors_states: float32 [2, 6, 2048], P(None, None, ('dp', 'tensor'))
- vectors_update: float32 [6, 2048], P(None, ('dp', 'tensor'))
Inputs may be any that keep to these rules, and one draw needn't show every extreme that they name: `lengths`: dp index i holds slots i * 3 to i * 3 + 2; a slot is empty (0) or holds one sequence of 128 to 512 tokens; every index holds at least one sequence, some index has all its slots filled, one of them with 512 tokens, and some index holds exactly one sequence. `projector_moments`: the roots of the second moments (index 1 of the first dimension) are positive. `shifts_moments`: the roots of the second moments are positive. `combiner_moments`: the roots of the second moments are positive. `expander_moments`: the roots of the second moments are positive. `offsets_moments`: the roots of the second moments are positive. `reducer_moments`: the roots of the second moments are positive. `vectors_moments`: the roots of the second moments are positive.
All inputs are finite; a program needn't handle non-finite values.
Results may differ from a plain program's by a relative error of at most 0.014.
The roundings to bfloat16 on the way count: a program that leaves them out, or rounds other values in their place, can miss the bound.
Values may be sent and summed in bfloat16 or wider, within the bound.
A program may use at most 320 MiB of HBM per device.

v0:
```python
import math
import jax
import jax.numpy as jnp
from jax import lax
from jax.sharding import PartitionSpec as P

HD = 256
ROT = 64
SEQ_LEN = 512
STEP = 10
layer_eps = 1e-05
adam_eps = 1e-08
beta_one = 0.9
beta_two = 0.95
learn_rate = 0.02
decay_rate = 0.01
rotary_base = 10000.0


def norm_layer(values, scale_row, shift_row):
    average = jnp.mean(values, axis=-1, keepdims=True)
    centred = values - average
    variance = jnp.mean(centred * centred, axis=-1, keepdims=True)
    return centred * lax.rsqrt(variance + layer_eps) * scale_row + shift_row


def exact_gelu(values):
    return jax.nn.gelu(values, approximate=False)


def rotary_tables():
    half_rot = ROT // 2
    frequency = jnp.exp(
        jnp.arange(half_rot, dtype=jnp.float32) * (-2.0 * math.log(rotary_base) / ROT)
    )
    angles = jnp.arange(SEQ_LEN, dtype=jnp.float32)[:, None] * frequency[None, :]
    return (jnp.cos(angles)[:, None, :], jnp.sin(angles)[:, None, :])


def rotate(values, cos_table, sin_table):
    half_rot = ROT // 2
    leading = values[..., :half_rot]
    trailing = values[..., half_rot:ROT]
    return jnp.concatenate(
        [
            leading * cos_table - trailing * sin_table,
            trailing * cos_table + leading * sin_table,
            values[..., ROT:],
        ],
        axis=-1,
    )


def allowed_mask(length):
    position = jnp.arange(SEQ_LEN)
    return (position[None, :] <= position[:, None]) & (position[None, :] < jnp.maximum(length, 1))


def contract_rows(left, right):
    return lax.dot_general(
        left, right, (((0,), (0,)), ((), ())), preferred_element_type=jnp.float32
    )


def contract_cols(left, right):
    return lax.dot_general(
        left, right, (((1,), (1,)), ((), ())), preferred_element_type=jnp.float32
    )


def masked_scores(query_rows, key_rows, length):
    scores = jnp.einsum(
        "qhd,khd->hqk", query_rows, key_rows, preferred_element_type=jnp.float32
    ) * HD ** (-0.5)
    return jnp.where(allowed_mask(length)[None], scores, -1e30)


def attend_forward(query_rows, key_rows, value_rows, length):
    scores = masked_scores(query_rows, key_rows, length)
    largest = jnp.max(scores, axis=-1, keepdims=True)
    powers = jnp.exp(scores - largest)
    row_total = jnp.sum(powers, axis=-1, keepdims=True)
    weights = (powers / row_total).astype(jnp.bfloat16)
    mixture = jnp.einsum("hqk,khd->qhd", weights, value_rows, preferred_element_type=jnp.float32)
    return (mixture.astype(jnp.bfloat16), (largest + jnp.log(row_total))[..., 0])


def attend_backward(query_rows, key_rows, value_rows, length, summary, incoming):
    scores = masked_scores(query_rows, key_rows, length)
    weights = jnp.exp(scores - summary[..., None])
    pushed = jnp.einsum("qhd,khd->hqk", incoming, value_rows, preferred_element_type=jnp.float32)
    inner_sum = jnp.sum(weights * pushed, axis=-1, keepdims=True)
    dscores = (weights * (pushed - inner_sum)).astype(jnp.bfloat16)
    score_scale = HD ** (-0.5)
    grad_query = (
        jnp.einsum("hqk,khd->qhd", dscores, key_rows, preferred_element_type=jnp.float32)
        * score_scale
    )
    grad_keys = (
        jnp.einsum("hqk,qhd->khd", dscores, query_rows, preferred_element_type=jnp.float32)
        * score_scale
    )
    grad_values = jnp.einsum(
        "hqk,qhd->khd", weights.astype(jnp.bfloat16), incoming, preferred_element_type=jnp.float32
    )
    return (grad_query, grad_keys, grad_values)


def forward_slot(pieces):
    query_rows, key_rows, value_rows, length = pieces
    return attend_forward(query_rows, key_rows, value_rows, length)


def backward_slot(pieces):
    query_rows, key_rows, value_rows, length, summary, incoming = pieces
    return attend_backward(query_rows, key_rows, value_rows, length, summary, incoming)


def adamw(master, moments, gradient):
    first_moment = beta_one * moments[0] + (1.0 - beta_one) * gradient
    root_moment = jnp.sqrt(
        beta_two * moments[1] * moments[1] + (1.0 - beta_two) * gradient * gradient
    )
    first_hat = first_moment / (1.0 - beta_one**STEP)
    root_hat = root_moment / math.sqrt(1.0 - beta_two**STEP)
    update = -learn_rate * (first_hat / (root_hat + adam_eps) + decay_rate * master)
    return (jnp.stack([first_moment, root_moment]), update)


def on_device(
    layer_input,
    cotangent,
    lengths,
    projector,
    projector_moments,
    shifts,
    shifts_moments,
    combiner,
    combiner_moments,
    expander,
    expander_moments,
    offsets,
    offsets_moments,
    reducer,
    reducer_moments,
    vectors,
    vectors_moments,
):
    entry, entry_shift, combine, expand, expand_shift, shrink = (
        lax.all_gather(projector.astype(jnp.bfloat16), "dp", axis=0, tiled=True),
        lax.all_gather(shifts.astype(jnp.bfloat16), "dp", axis=1, tiled=True),
        lax.all_gather(combiner.astype(jnp.bfloat16), "dp", axis=1, tiled=True),
        lax.all_gather(expander.astype(jnp.bfloat16), "dp", axis=0, tiled=True),
        lax.all_gather(offsets.astype(jnp.bfloat16), "dp", axis=1, tiled=True),
        lax.all_gather(reducer.astype(jnp.bfloat16), "dp", axis=1, tiled=True),
    )
    full_vectors = lax.all_gather(
        vectors.astype(jnp.bfloat16), ("dp", "tensor"), axis=1, tiled=True
    ).astype(jnp.float32)
    slot_count = lengths.shape[0]
    row_count = slot_count * SEQ_LEN
    local_heads = entry.shape[1] // (3 * HD)
    cos_table, sin_table = rotary_tables()
    inputs = layer_input.astype(jnp.float32)
    first_norm, first_back = jax.vjp(norm_layer, inputs, full_vectors[0], full_vectors[1])
    normed_one = first_norm.astype(jnp.bfloat16)
    packed = jnp.dot(normed_one, entry, preferred_element_type=jnp.float32) + entry_shift.astype(
        jnp.float32
    ).reshape(-1)
    packed = packed.reshape(slot_count, SEQ_LEN, local_heads, 3, HD)
    query_rows = rotate(packed[:, :, :, 0], cos_table, sin_table).astype(jnp.bfloat16)
    key_rows = rotate(packed[:, :, :, 1], cos_table, sin_table).astype(jnp.bfloat16)
    value_rows = packed[:, :, :, 2].astype(jnp.bfloat16)
    mixture, summary = lax.map(forward_slot, (query_rows, key_rows, value_rows, lengths))
    attended = mixture.reshape(row_count, local_heads * HD)
    second_norm, second_back = jax.vjp(norm_layer, inputs, full_vectors[2], full_vectors[3])
    normed_two = second_norm.astype(jnp.bfloat16)
    hidden = jnp.dot(normed_two, expand, preferred_element_type=jnp.float32) + expand_shift.astype(
        jnp.float32
    ).reshape(-1)
    activated, gelu_back = jax.vjp(exact_gelu, hidden)
    activated = activated.astype(jnp.bfloat16)
    partial_sum = jnp.dot(attended, combine, preferred_element_type=jnp.float32) + jnp.dot(
        activated, shrink, preferred_element_type=jnp.float32
    )
    summed = lax.psum_scatter(
        partial_sum.astype(jnp.bfloat16), "tensor", scatter_dimension=1, tiled=True
    ).astype(jnp.float32)
    own_width = summed.shape[1]
    own_start = lax.axis_index("tensor") * own_width
    own_input = lax.dynamic_slice_in_dim(inputs, own_start, own_width, 1)
    own_bias = lax.dynamic_slice_in_dim(full_vectors[4] + full_vectors[5], own_start, own_width, 0)
    live_rows = (
        (jnp.arange(SEQ_LEN)[None, :] < lengths[:, None]).astype(jnp.float32).reshape(row_count, 1)
    )
    layer_output = (live_rows * (own_input + summed + own_bias)).astype(jnp.bfloat16)
    upstream_float = cotangent.astype(jnp.float32) * live_rows
    upstream = upstream_float.astype(jnp.bfloat16)
    dactivated = contract_cols(upstream, shrink)
    dhidden = gelu_back(dactivated)[0].astype(jnp.bfloat16)
    expand_local = contract_rows(normed_two, dhidden)
    expand_bias_local = jnp.sum(dhidden.astype(jnp.float32), axis=0).reshape(expand_shift.shape)
    shrink_local = contract_rows(activated, upstream)
    dnormed_two = contract_cols(dhidden, expand)
    dattended = contract_cols(upstream, combine).astype(jnp.bfloat16)
    combine_local = contract_rows(attended, upstream)
    incoming = dattended.reshape(slot_count, SEQ_LEN, local_heads, HD)
    grad_query, grad_keys, grad_values = lax.map(
        backward_slot, (query_rows, key_rows, value_rows, lengths, summary, incoming)
    )
    grad_query = rotate(grad_query, cos_table, -sin_table)
    grad_keys = rotate(grad_keys, cos_table, -sin_table)
    dpacked = (
        jnp.stack([grad_query, grad_keys, grad_values], axis=3)
        .reshape(row_count, 3 * local_heads * HD)
        .astype(jnp.bfloat16)
    )
    entry_local = contract_rows(normed_one, dpacked)
    entry_bias_local = jnp.sum(dpacked.astype(jnp.float32), axis=0).reshape(entry_shift.shape)
    dnormed_one = contract_cols(dpacked, entry)
    dinput_one, dscale_one, dshift_one = first_back(dnormed_one)
    dinput_two, dscale_two, dshift_two = second_back(dnormed_two)
    bias_total = jnp.sum(upstream_float, axis=0)
    vector_local = jnp.stack(
        [dscale_one, dshift_one, dscale_two, dshift_two, bias_total, bias_total]
    )
    (
        entry_share,
        entry_bias_share,
        combine_share,
        vector_share,
        expand_share,
        expand_bias_share,
        shrink_share,
    ) = (
        lax.psum_scatter(entry_local, "dp", scatter_dimension=0, tiled=True),
        lax.psum_scatter(entry_bias_local, "dp", scatter_dimension=1, tiled=True),
        lax.psum_scatter(combine_local, "dp", scatter_dimension=1, tiled=True),
        lax.psum_scatter(vector_local, "dp", scatter_dimension=1, tiled=True),
        lax.psum_scatter(expand_local, "dp", scatter_dimension=0, tiled=True),
        lax.psum_scatter(expand_bias_local, "dp", scatter_dimension=1, tiled=True),
        lax.psum_scatter(shrink_local, "dp", scatter_dimension=1, tiled=True),
    )
    input_part, norm_share = (
        lax.psum_scatter(
            (dinput_one + dinput_two).astype(jnp.bfloat16),
            "tensor",
            scatter_dimension=1,
            tiled=True,
        ).astype(jnp.float32),
        lax.psum_scatter(
            vector_share[:4].astype(jnp.bfloat16), "tensor", scatter_dimension=1, tiled=True
        ).astype(jnp.float32),
    )
    own_cot = lax.dynamic_slice_in_dim(upstream_float, own_start, own_width, 1)
    input_gradient = (input_part + own_cot).astype(jnp.bfloat16)
    piece_width = vector_share.shape[1] // lax.axis_size("tensor")
    bias_share = lax.dynamic_slice_in_dim(
        vector_share[4:], lax.axis_index("tensor") * piece_width, piece_width, 1
    )
    vector_gradient = jnp.concatenate([norm_share, bias_share], axis=0)
    projector_states, projector_update = adamw(projector, projector_moments, entry_share)
    shifts_states, shifts_update = adamw(shifts, shifts_moments, entry_bias_share)
    combiner_states, combiner_update = adamw(combiner, combiner_moments, combine_share)
    expander_states, expander_update = adamw(expander, expander_moments, expand_share)
    offsets_states, offsets_update = adamw(offsets, offsets_moments, expand_bias_share)
    reducer_states, reducer_update = adamw(reducer, reducer_moments, shrink_share)
    vectors_states, vectors_update = adamw(vectors, vectors_moments, vector_gradient)
    return (
        layer_output,
        input_gradient,
        entry_share,
        projector_states,
        projector_update,
        entry_bias_share,
        shifts_states,
        shifts_update,
        combine_share,
        combiner_states,
        combiner_update,
        expand_share,
        expander_states,
        expander_update,
        expand_bias_share,
        offsets_states,
        offsets_update,
        shrink_share,
        reducer_states,
        reducer_update,
        vector_gradient,
        vectors_states,
        vectors_update,
    )


def solution(mesh):
    placed = (
        P("dp", None),
        P("dp", None),
        P("dp"),
        P("dp", "tensor"),
        P(None, "dp", "tensor"),
        P("tensor", "dp"),
        P(None, "tensor", "dp"),
        P("tensor", "dp"),
        P(None, "tensor", "dp"),
        P("dp", "tensor"),
        P(None, "dp", "tensor"),
        P("tensor", "dp"),
        P(None, "tensor", "dp"),
        P("tensor", "dp"),
        P(None, "tensor", "dp"),
        P(None, ("dp", "tensor")),
        P(None, None, ("dp", "tensor")),
    )
    return jax.shard_map(
        on_device,
        mesh=mesh,
        in_specs=placed,
        out_specs=(
            P("dp", "tensor"),
            P("dp", "tensor"),
            P("dp", "tensor"),
            P(None, "dp", "tensor"),
            P("dp", "tensor"),
            P("tensor", "dp"),
            P(None, "tensor", "dp"),
            P("tensor", "dp"),
            P("tensor", "dp"),
            P(None, "tensor", "dp"),
            P("tensor", "dp"),
            P("dp", "tensor"),
            P(None, "dp", "tensor"),
            P("dp", "tensor"),
            P("tensor", "dp"),
            P(None, "tensor", "dp"),
            P("tensor", "dp"),
            P("tensor", "dp"),
            P(None, "tensor", "dp"),
            P("tensor", "dp"),
            P(None, ("dp", "tensor")),
            P(None, None, ("dp", "tensor")),
            P(None, ("dp", "tensor")),
        ),
        check_vma=False,
    )
```

profile of v0, /device:TPU:0, one launch (start us, length us, event | category | flops | bytes accessed | tf_op | source)
XLA Modules:
  0.0 1193.2 jit_solution(17004085662014109550)
XLA Ops:
  23.0 69.1 %all-gather = bf16[32,64,6]{1,2,0:T(8,128)(2,1)S(1)} all-gather(bf16[1,64,6]{1,2,0:T(8,128)(2,1)S(1)} %convert_bitcast_fusion.1), channel_id=1, replica_groups=mesh['dp'=8,'tensor'=4] {'dp','tensor'}, dimensions={0}, use_global_device_ids=true | all-gather | bytes 25344 | tf_op jit(solution)/shard_map/all_gather | solution.py:157
  112.2 16.0 %convolution_add_fusion = f32[1536,1536]{1,0:T(8,128)} fusion(bf16[2048,1536]{1,0:T(8,128)(2,1)} %all-gather.7.cloned.1.call-done, f32[1536]{0:T(1024)S(1)} %reshape.413, bf16[1536,2048]{1,0:T(8,128)(2,1)} %param.21, f32[2048]{0:T(1024)S(1)} %bitcast.340, f32[2048]{0:T(1024)S(1)} %bitcast.321, f32[1536]{0:T(1024)S(1)} %fusion.64, ...), kind=kOutput, calls=%fused_computation.89 | convolution fusion | flops 9684910080 | bytes 22054912 | tf_op jit(solution)/shard_map/dot_general | solution.py:167
  128.2 15.8 %reshape.403 = f32[3,512,2,3,256]{4,3,2,1,0:T(4,128)} reshape(f32[1536,1536]{1,0:T(8,128)} %convolution_add_fusion) | data formatting | bytes 18874368 | tf_op jit(solution)/shard_map/reshape | solution.py:170
  158.3 13.5 %fusion.105 = (f32[3,512,2,1,256]{4,3,2,1,0:T(1,128)S(1)}, f32[3,512,2,1,256]{4,3,2,1,0:T(1,128)S(1)}) fusion(f32[3,512,2,3,256]{4,3,2,1,0:T(4,128)} %reshape.403), kind=kLoop, calls=%fused_computation.225 | loop fusion | bytes 12582912 | tf_op jit(solution)/shard_map/slice | solution.py:172
  195.9 23.0 %while.26 = (s32[]{:T(128)}, bf16[3,512,2,256]{3,2,1,0:T(2,128)(2,1)}, f32[3,2,512]{2,1,0:T(2,128)}, bf16[3,512,2,256]{1,3,2,0:T(8,128)(2,1)}, s32[3]{0:T(128)S(...) while((s32[]{:T(128)}, ...), condition=%wide.region_5.6_spmd, body=%wide.region_2.5_spmd.sunk | while | flops 543948288 | bytes 11569293 | solution.py:174
  230.4 48.3 %multiply_convert_fusion.1 = (bf16[1536,2048]{1,0:T(8,128)(2,1)S(1)}, f32[1536,2048]{1,0:T(8,128)}, f32[1536,2048]{1,0:T(8,128)}) fusion(f32[2048]{0:T(1024)S(1)} %bitcast.342, bf16[2048,2048]{1,0:T(8,128)(2,1)} %all-gather.11.cloned.1.call-done, bf16[1536,2048]{1,0:T(8,128)(2,1)} %param.21, f32[2048]{0:T(1024)S(1)} %bitcast.338, f32[2048]{0:T(1024)S(1)} %bitcast.316, ...), kind=kOutput, calls=%fused_computation.70 | convolution fusion | flops 13111394304 | bytes 46174208 | tf_op jit(solution)/shard_map/dot_general | solution.py:178
  281.4 19.6 %fusion.93 = f32[2048,2048]{1,0:T(8,128)} fusion(bf16[1536,2048]{1,0:T(8,128)(2,1)S(1)} %get-tuple-element.368, f32[1536]{0:T(1024)S(1)} %reshape.412, bf16[1536,2048]{1,0:T(8,128)(2,1)} %param.22), kind=kOutput, calls=%fused_computation.220 | convolution fusion | flops 12894339072 | bytes 29366272 | tf_op jit(solution)/shard_map/dot_general | solution.py:60
  305.2 109.2 %reduce-scatter.27.cloned.1.call-done = f32[2048,256]{1,0:T(8,128)} async-done(((f32[2048,2048]{1,0:T(8,128)}), f32[2048,256]{1,0:T(8,128)}) %reduce-scatter.27.cloned.1.call-update) | async-done | bytes 2097168 | tf_op jit(solution)/shard_map/reduce_scatter | solution.py:242
  456.3 33.5 %while.27 = (s32[]{:T(128)}, f32[3,512,2,256]{1,3,2,0:T(8,128)}, f32[3,512,2,256]{1,3,2,0:T(8,128)}, bf16[3,512,2,256]{1,3,2,0:T(8,128)(2,1)}, bf16[3,512,2,256]...) while((s32[]{:T(128)}, f32[3,512,2,256]{1,3,2,0:T(8,128)}, ...), condition=%wide.region_9.10_spmd, body=%wide.region_7.9_spmd.sunk | while | flops 1347943936 | bytes 36724960 | solution.py:208
  522.1 26.9 %convert_reduce_fusion = (f32[2048]{0:T(1024)S(1)}, bf16[1536,2048]{1,0:T(8,128)(2,1)}) fusion(f32[1536,2048]{1,0:T(8,128)} %get-tuple-element.369, bf16[2048,2048]{1,0:T(8,128)(2,1)} %all-gather.13.cloned.1.call-done, f32[1536]{0:T(1024)S(1)} %reshape.412, bf16[1536,2048]{1,0:T(8,128)(2,1)} %param.22, f32[1536,2048]{1,0:T(8,128)} %get-tuple-element.429, ...), kind=kOutput, calls=%fused_computation.63 | convolution fusion | flops 12947814400 | bytes 46159872 | tf_op jit(solution)/shard_map/dot_general | solution.py:66
  549.0 19.2 %fusion.109 = f32[1536,2048]{1,0:T(8,128)} fusion(bf16[1536,2048]{1,0:T(8,128)(2,1)} %get-tuple-element.432, bf16[2048,2048]{1,0:T(8,128)(2,1)} %all-gather.11.cloned.1.call-done), kind=kOutput, calls=%fused_computation.229 | convolution fusion | flops 12884901888 | bytes 27262976 | tf_op jit(solution)/shard_map/dot_general | solution.py:66
  568.3 22.1 %fusion.103 = (f32[2048]{0:T(1024)S(1)}, f32[1536]{0:T(1024)S(1)}, f32[1536]{0:T(1024)S(1)}, f32[2048]{0:T(1024)S(1)}, f32[1536,2048]{1,0:T(8,128)}) fusion(f32[2048]{0:T(1024)S(1)} %bitcast.322, f32[1536]{0:T(1024)S(1)} %copy-done.23, bf16[1536,2048]{1,0:T(8,128)(2,1)} %param.21, f32[1536,2048]{1,0:T(8,128)} %fusion.109, f32[2048]{0:T(1024)S(1)} %bitcast.317, ...), kind=kOutput, calls=%fused_computation.224 | convolution fusion | flops 9695125504 | bytes 42518528 | tf_op jit(solution)/shard_map/dot_general | solution.py:66
  590.5 14.1 %multiply_reduce_fusion.1 = (f32[2048]{0:T(1024)S(1)}, f32[1536]{0:T(1024)S(1)}, f32[1536]{0:T(1024)S(1)}, f32[2048]{0:T(1024)S(1)}) fusion(f32[1536,2048]{1,0:T(8,128)} %fusion.109, bf16[1536,2048]{1,0:T(8,128)(2,1)} %param.21, f32[1536]{0:T(1024)S(1)} %copy-done.31, f32[1536]{0:T(1024)S(1)} %copy-done.23, f32[1536]{0:T(1024)S(1)} %get-tuple-element.413, ...), kind=kLoop, calls=%fused_computation.61 | loop fusion | flops 59761664 | bytes 31526912 | tf_op jit(solution)/shard_map/transpose(jvp())/reduce_sum | solution.py:24
  606.6 16.7 %fusion.90 = f32[2048,1536]{1,0:T(8,128)} fusion(bf16[1536,1536]{1,0:T(8,128)(2,1)} %convert_element_type.139, bf16[1536,2048]{1,0:T(8,128)(2,1)} %param.21, f32[2048]{0:T(1024)S(1)} %bitcast.341, f32[2048]{0:T(1024)S(1)} %bitcast.324, f32[1536]{0:T(1024)S(1)} %copy-done.31, f32[1536]{0:T(1024)S(1)} %copy-done.23), kind=kOutput, calls=%fused_computation.217 | convolution fusion | flops 9682550784 | bytes 23621632 | tf_op jit(solution)/shard_map/dot_general | solution.py:60
  624.5 14.5 %reduce-scatter.29.cloned.1.call-done = f32[6,256]{1,0:T(8,128)} async-done(((f32[6,2048]{1,0:T(8,128)}), f32[6,256]{1,0:T(8,128)}) %reduce-scatter.29.cloned.1.call-update) | async-done | bytes 6160 | tf_op jit(solution)/shard_map/reduce_scatter | solution.py:239
  640.5 16.2 %add_convert_fusion = bf16[1536,2048]{1,0:T(8,128)(2,1)} fusion(f32[1536]{0:T(1024)S(1)} %negate_multiply_fusion.1, f32[1536]{0:T(1024)S(1)} %negate_multiply_fusion.2, f32[1536]{0:T(1024)S(1)} %get-tuple-element.412, f32[1536]{0:T(1024)S(1)} %copy-done.23, bf16[1536,2048]{1,0:T(8,128)(2,1)} %param.21, f32[1536]{0:T(1024)S(1)} %copy-done.31, ...), kind=kLoop, calls=%fused_computation.64 | loop fusion | flops 50331648 | bytes 37801984 | tf_op jit(solution)/shard_map/convert_element_type | solution.py:246
  666.0 21.3 %add_convert_fusion.2 = bf16[1536,2048]{1,0:T(8,128)(2,1)} fusion(f32[1536,2048]{1,0:T(8,128)} %fusion.108, bf16[1536,2048]{1,0:T(8,128)(2,1)} %copy-done.52, bf16[2048,2048]{1,0:T(8,128)(2,1)} %all-gather.13.cloned.1.call-done), kind=kOutput, calls=%fused_computation.69 | convolution fusion | flops 12891193344 | bytes 33554432 | tf_op jit(solution)/shard_map/dot_general | solution.py:183
  687.9 24.6 %fusion.88 = f32[2048,2048]{1,0:T(8,128)} fusion(bf16[1536,2048]{1,0:T(8,128)(2,1)} %get-tuple-element.432, bf16[1536,2048]{1,0:T(8,128)(2,1)} %param.21, f32[2048]{0:T(1024)S(1)} %bitcast.339, f32[2048]{0:T(1024)S(1)} %bitcast.320, f32[1536]{0:T(1024)S(1)} %copy-done.31, f32[1536]{0:T(1024)S(1)} %copy-done.23), kind=kOutput, calls=%fused_computation.215 | convolution fusion | flops 12903776256 | bytes 29388800 | tf_op jit(solution)/shard_map/dot_general | solution.py:60
  725.7 47.3 %reduce-scatter.21.cloned.1.call-done = f32[256,1536]{1,0:T(8,128)} async-done(((f32[2048,1536]{1,0:T(8,128)}), f32[256,1536]{1,0:T(8,128)}) %reduce-scatter.21.cloned.1.call-update) | async-done | bytes 1572880 | tf_op jit(solution)/shard_map/reduce_scatter | solution.py:236
  783.3 27.3 %reduce-scatter.33.cloned.1.call-done = f32[128,2]{1,0:T(8,128)} async-done(((f32[1024,2]{1,0:T(8,128)}), f32[128,2]{1,0:T(8,128)}) %reduce-scatter.33.cloned.1.call-update) | async-done | bytes 1040
  813.5 19.2 %reduce-scatter.35.cloned.1.call-done = bf16[64,4]{1,0:T(8,128)(2,1)} async-done(((bf16[256,4]{1,0:T(8,128)(2,1)}), bf16[64,4]{1,0:T(8,128)(2,1)}) %reduce-scatter.35.cloned.1.call-update) | async-done | bytes 528
  834.8 109.1 %reduce-scatter.19.cloned.1.call-done = bf16[1536,512]{1,0:T(8,128)(2,1)} async-done(((bf16[1536,2048]{1,0:T(8,128)(2,1)}), bf16[1536,512]{1,0:T(8,128)(2,1)}) %reduce-scatter.19.cloned.1.call-update) | async-done | bytes 1572880 | tf_op jit(solution)/shard_map/reduce_scatter | solution.py:245
  947.9 109.6 %reduce-scatter.17.cloned.1.call-done = bf16[1536,512]{1,0:T(8,128)(2,1)} async-done(((bf16[1536,2048]{1,0:T(8,128)(2,1)}), bf16[1536,512]{1,0:T(8,128)(2,1)}) %reduce-scatter.17.cloned.1.call-update) | async-done | bytes 1572880 | tf_op jit(solution)/shard_map/reduce_scatter | solution.py:186
  1061.5 116.7 %reduce-scatter.25.cloned.1.call-done = f32[256,2048]{1,0:T(8,128)} async-done(((f32[2048,2048]{1,0:T(8,128)}), f32[256,2048]{1,0:T(8,128)}) %reduce-scatter.25.cloned.1.call-update) | async-done | bytes 2097168 | tf_op jit(solution)/shard_map/reduce_scatter | solution.py:240
  (300 shorter events, 278.1 us)
Async XLA Ops:
  7.2 104.9 %all-gather.7.cloned.1.call-start = ((), (), s32[]{:S(2)}) async-start(), calls=%async_computation.10 | async-start | bytes 7077888 | tf_op jit(solution)/shard_map/all_gather | solution.py:150
  9.7 220.7 %all-gather.11.cloned.1.call-start = ((), (), s32[]{:S(2)}) async-start(), calls=%async_computation.12 | async-start | bytes 9437184 | tf_op jit(solution)/shard_map/all_gather | solution.py:153
  12.5 288.6 %reduce-scatter.23.cloned.1.call-start = ((), (), s32[]{:S(2)}) async-start(), calls=%async_computation.17 | async-start | bytes 4718592 | tf_op jit(solution)/shard_map/reduce_scatter | solution.py:238
  92.2 429.9 %copy-start.28 = (f32[1536]{0:T(1024)}, f32[1536]{0:T(1024)S(1)}, u32[]{:S(2)}) copy-start(f32[1536]{0:T(1024)S(1)} %reshape.412) | copy-start | bytes 18436
  105.0 125.4 %copy-start.22 = (f32[1536]{0:T(1024)}, f32[1536]{0:T(1024)S(1)}, u32[]{:S(2)}) copy-start(f32[1536]{0:T(1024)S(1)} %broadcast_multiply_fusion) | copy-start | bytes 18436
  109.6 120.8 %copy-start.30 = (f32[1536]{0:T(1024)}, f32[1536]{0:T(1024)S(1)}, u32[]{:S(2)}) copy-start(f32[1536]{0:T(1024)S(1)} %fusion.64) | copy-start | bytes 18436
  112.1 118.3 %copy-start.24 = (f32[1,2048]{1,0:T(1,128)}, f32[1,2048]{1,0:T(1,128)S(1)}, u32[]{:S(2)}) copy-start(f32[1,2048]{1,0:T(1,128)S(1)} %get-tuple-element.409) | copy-start | bytes 24580
  112.1 118.3 %copy-start.37 = (f32[1,2048]{1,0:T(1,128)}, f32[1,2048]{1,0:T(1,128)S(1)}, u32[]{:S(2)}) copy-start(f32[1,2048]{1,0:T(1,128)S(1)} %get-tuple-element.408) | copy-start | bytes 24580
  230.3 184.0 %reduce-scatter.27.cloned.1.call-start = ((), (), s32[]{:S(2)}) async-start(), calls=%async_computation.19 | async-start | bytes 18874368 | tf_op jit(solution)/shard_map/reduce_scatter | solution.py:242
  301.0 143.2 %all-gather.9.cloned.1.call-start = ((), (), s32[]{:S(2)}) async-start(), calls=%async_computation.11 | async-start | bytes 2359296 | tf_op jit(solution)/shard_map/all_gather | solution.py:152
  305.1 116.3 %copy-start.10 = (f32[512,32]{1,0:T(8,128)S(1)}, f32[512,32]{1,0:T(8,128)}, u32[]{:S(2)}) copy-start(f32[512,32]{1,0:T(8,128)} %copy-done.9) | copy-start | bytes 196612
  305.1 116.4 %copy-start.20 = (f32[512,32]{1,0:T(8,128)S(1)}, f32[512,32]{1,0:T(8,128)}, u32[]{:S(2)}) copy-start(f32[512,32]{1,0:T(8,128)} %get-tuple-element.426) | copy-start | bytes 196612
  305.1 217.0 %all-gather.13.cloned.1.call-start = ((), (), s32[]{:S(2)}) async-start(), calls=%async_computation.13 | async-start | bytes 9437184 | tf_op jit(solution)/shard_map/all_gather | solution.py:155
  421.3 217.7 %reduce-scatter.29.cloned.1.call-start = ((), (), s32[]{:S(2)}) async-start(), calls=%async_computation.20 | async-start | bytes 73728 | tf_op jit(solution)/shard_map/reduce_scatter | solution.py:239
  605.3 118.3 %reduce-scatter.31.cloned.1.call-start = ((), (), s32[]{:S(2)}) async-start(), calls=%async_computation.21 | async-start | bytes 442368
  606.6 166.4 %reduce-scatter.21.cloned.1.call-start = ((), (), s32[]{:S(2)}) async-start(), calls=%async_computation.16 | async-start | bytes 14155776 | tf_op jit(solution)/shard_map/reduce_scatter | solution.py:236
  623.3 187.2 %reduce-scatter.33.cloned.1.call-start = ((), (), s32[]{:S(2)}) async-start(), calls=%async_computation.22 | async-start | bytes 589824
  624.5 208.3 %reduce-scatter.35.cloned.1.call-start = ((), (), s32[]{:S(2)}) async-start(), calls=%async_computation.23 | async-start | bytes 81920
  640.5 303.4 %reduce-scatter.19.cloned.1.call-start = ((), (), s32[]{:S(2)}) async-start(), calls=%async_computation.15 | async-start | bytes 7864320 | tf_op jit(solution)/shard_map/reduce_scatter | solution.py:245
  656.7 400.8 %reduce-scatter.17.cloned.1.call-start = ((), (), s32[]{:S(2)}) async-start(), calls=%async_computation.14 | async-start | bytes 7864320 | tf_op jit(solution)/shard_map/reduce_scatter | solution.py:186
  687.2 490.9 %reduce-scatter.25.cloned.1.call-start = ((), (), s32[]{:S(2)}) async-start(), calls=%async_computation.18 | async-start | bytes 18874368 | tf_op jit(solution)/shard_map/reduce_scatter | solution.py:240
  783.3 274.2 %copy-start.29 = (f32[1536]{0:T(1024)S(1)}, f32[1536]{0:T(1024)}, u32[]{:S(2)}) copy-start(f32[1536]{0:T(1024)} %copy-done.28) | copy-start | bytes 18436
  811.5 250.0 %copy-start.42 = (f32[2,128]{1,0:T(2,128)}, f32[2,128]{1,0:T(2,128)S(1)}, u32[]{:S(2)}) copy-start(f32[2,128]{1,0:T(2,128)S(1)} %copy.190) | copy-start | bytes 3076
  947.9 230.3 %copy-start.5 = (f32[256,2048]{1,0:T(8,128)S(1)}, f32[256,2048]{1,0:T(8,128)}, u32[]{:S(2)}) copy-start(f32[256,2048]{1,0:T(8,128)} %param.30) | copy-start | bytes 6291460
  (47 other events, 968.5 us)
Sparse Core Ops, SparseCore 0:
  10.5 48.2 all-gather.6
  61.2 54.3 all-gather.10
  230.4 48.3 reduce-scatter.22
  301.1 113.1 reduce-scatter.26
  416.1 28.1 all-gather.8
  446.5 55.8 all-gather.12
  605.5 33.4 reduce-scatter.28
  642.6 33.8 reduce-scatter.30
  680.6 92.2 reduce-scatter.20
  776.4 34.0 reduce-scatter.32
  813.4 19.2 reduce-scatter.34
  834.9 108.9 reduce-scatter.18
  946.1 111.2 reduce-scatter.16
  1061.5 116.6 reduce-scatter.24
where the time goes:
time: 1200 us; the launch traced here: 1190 us
  waiting for transfers between devices  565 us (47%)
  matrix products  267 us (22%)
  other arithmetic  130 us (11%)
  local copies, waits for them, and re-layouts  123 us (10%)
  blocking collectives  88.4 us (7%)
  between operations  14.8 us (1%)
    reduce_scatter x1, waiting for transfers between devices, on_device(): lax.psum_scatter(expand_local, 'dp', scatter_dimension=0, tiled=True)  117 us
    reduce_scatter x1, waiting for transfers between devices, on_device(): lax.psum_scatter(partial_sum.astype(jnp.bfloat16), 'tensor', scatter_dime...  110 us
    reduce_scatter x1, waiting for transfers between devices, on_device(): lax.psum_scatter(shrink_local, 'dp', scatter_dimension=1, tiled=True)  109 us
    reduce_scatter x1, waiting for transfers between devices, on_device(): lax.psum_scatter((dinput_one + dinput_two).astype(jnp.bfloat16), 'tensor'...  109 us
    dot_general x4, matrix products, contract_cols(): lax.dot_general(left, right, (((1,), (1,)), ((), ())), preferred_element_...  76.3 us
    all_gather x1, blocking collectives, on_device(): lax.all_gather(vectors.astype(jnp.bfloat16), ('dp', 'tensor'), axis=1, ti...  69.1 us
    dot_general x4, matrix products, contract_rows(): lax.dot_general(left, right, (((0,), (0,)), ((), ())), preferred_element_...  68.8 us
    dot_general x1, matrix products, on_device(): jnp.dot(normed_two, expand, preferred_element_type=jnp.float32)  48.3 us
  transfers between devices with their start and end apart: 14, of which 9 were waited for; matrix products, arithmetic and copies ran while one was open for 35% of the time, Pallas kernels for 0%

commit v1 on v0

--- a/solution.py
+++ b/solution.py
@@ -1,8 +1,10 @@
+import functools
 import math
 import jax
 import jax.numpy as jnp
 from jax import lax
 from jax.sharding import PartitionSpec as P
+from jax.lax import axis_index, axis_size, ppermute
 
 HD = 256
 ROT = 64
@@ -15,6 +17,24 @@
 learn_rate = 0.02
 decay_rate = 0.01
 rotary_base = 10000.0
+
+
+def _choose_loads(block_in, along_dim):
+    all_rows = axis_size(("dp", "tensor"))
+    spare = axis_index(("dp", "tensor"))
+    main, q_next = (all_rows, spare)
+    upper, next_value = (block_in, 1)
+    while next_value < main:
+        part_next = tuple(((src_i, src_i ^ next_value) for src_i in range(main)))
+        g_now = ppermute(upper, axis_name=("dp", "tensor"), perm=part_next)
+        current_value = jnp.concatenate([upper, g_now], along_dim)
+        high = jnp.concatenate([g_now, upper], along_dim)
+        upper = jnp.where(q_next & next_value == 0, current_value, high)
+        next_value = 2 * next_value
+    return upper
+
+
+answer_the_block = functools.partial(_choose_loads, along_dim=1)
 
 
 def norm_layer(values, scale_row, shift_row):
@@ -154,9 +174,7 @@
         lax.all_gather(offsets.astype(jnp.bfloat16), "dp", axis=1, tiled=True),
         lax.all_gather(reducer.astype(jnp.bfloat16), "dp", axis=1, tiled=True),
     )
-    full_vectors = lax.all_gather(
-        vectors.astype(jnp.bfloat16), ("dp", "tensor"), axis=1, tiled=True
-    ).astype(jnp.float32)
+    full_vectors = answer_the_block(vectors.astype(jnp.bfloat16)).astype(jnp.float32)
     slot_count = lengths.shape[0]
     row_count = slot_count * SEQ_LEN
     local_heads = entry.shape[1] // (3 * HD)

time: 1200 us -> 1150 us (0.958)
  blocking collectives: 88.4 us -> 18.4 us
  waiting for transfers between devices: 565 us -> 579 us
    all_gather x1 -> x0, blocking collectives: 69.1 us -> none  [on_device(): lax.all_gather(vectors.astype(jnp.bfloat16), ('dp', 'tensor'), axis=1, ti...]
  transfers between devices with their start and end apart: 14 -> 19, of which waited for: 9 -> 12; matrix products, arithmetic and copies ran while one was open for 35% -> 36% of each run, Pallas kernels for 0% -> 0%
where the time goes in v1:
time: 1150 us; the launch traced here: 1140 us
  waiting for transfers between devices  579 us (50%)
  matrix products  266 us (23%)
  other arithmetic  128 us (11%)
  local copies, waits for them, and re-layouts  123 us (11%)
  blocking collectives  18.4 us (2%)
  between operations  14.8 us (1%)
    reduce_scatter x1, waiting for transfers between devices, on_device(): lax.psum_scatter(expand_local, 'dp', scatter_dimension=0, tiled=True)  117 us
    reduce_scatter x1, waiting for transfers between devices, on_device(): lax.psum_scatter(shrink_local, 'dp', scatter_dimension=1, tiled=True)  113 us
    reduce_scatter x1, waiting for transfers between devices, on_device(): lax.psum_scatter(partial_sum.astype(jnp.bfloat16), 'tensor', scatter_dime...  110 us
    reduce_scatter x1, waiting for transfers between devices, on_device(): lax.psum_scatter((dinput_one + dinput_two).astype(jnp.bfloat16), 'tensor'...  109 us
    dot_general x4, matrix products, contract_cols(): lax.dot_general(left, right, (((1,), (1,)), ((), ())), preferred_element_...  76.4 us
    dot_general x4, matrix products, contract_rows(): lax.dot_general(left, right, (((0,), (0,)), ((), ())), preferred_element_...  68.8 us
    dot_general x1, matrix products, on_device(): jnp.dot(normed_two, expand, preferred_element_type=jnp.float32)  47.7 us
    reduce_scatter x1, waiting for transfers between devices, on_device(): lax.psum_scatter(entry_local, 'dp', scatter_dimension=0, tiled=True)  47.3 us
  transfers between devices with their start and end apart: 19, of which 12 were waited for; matrix products, arithmetic and copies ran while one was open for 36% of the time, Pallas kernels for 0%

profile of v1, /device:TPU:0, one launch (start us, length us, event | category | flops | bytes accessed | tf_op | source)
XLA Modules:
  0.0 1142.9 jit_solution(3433127459435759473)
XLA Ops:
  59.0 15.9 %convolution_add_fusion = f32[1536,1536]{1,0:T(8,128)} fusion(bf16[2048,1536]{1,0:T(8,128)(2,1)} %all-gather.6.cloned.1.call-done, f32[1536]{0:T(1024)S(1)} %reshape.413, bf16[1536,2048]{1,0:T(8,128)(2,1)} %param.21, f32[2048]{0:T(1024)S(1)} %bitcast.332, f32[2048]{0:T(1024)S(1)} %bitcast.313, f32[1536]{0:T(1024)S(1)} %fusion.65, ...), kind=kOutput, calls=%fused_computation.89 | convolution fusion | flops 9684910080 | bytes 22054912 | tf_op jit(solution)/shard_map/dot_general | solution.py:185
  74.9 15.8 %reshape.403 = f32[3,512,2,3,256]{4,3,2,1,0:T(4,128)} reshape(f32[1536,1536]{1,0:T(8,128)} %convolution_add_fusion) | data formatting | bytes 18874368 | tf_op jit(solution)/shard_map/reshape | solution.py:188
  105.1 13.3 %fusion.106 = (f32[3,512,2,1,256]{4,3,2,1,0:T(1,128)S(1)}, f32[3,512,2,1,256]{4,3,2,1,0:T(1,128)S(1)}) fusion(f32[3,512,2,3,256]{4,3,2,1,0:T(4,128)} %reshape.403), kind=kLoop, calls=%fused_computation.229 | loop fusion | bytes 12582912 | tf_op jit(solution)/shard_map/slice | solution.py:190
  142.4 23.0 %while.26 = (s32[]{:T(128)}, bf16[3,512,2,256]{3,2,1,0:T(2,128)(2,1)}, f32[3,2,512]{2,1,0:T(2,128)}, bf16[3,512,2,256]{1,3,2,0:T(8,128)(2,1)}, s32[3]{0:T(128)S(...) while((s32[]{:T(128)}, ...), condition=%wide.region_5.6_spmd, body=%wide.region_2.5_spmd.sunk | while | flops 543948288 | bytes 11569293 | solution.py:192
  176.9 47.7 %multiply_convert_fusion.1 = (bf16[1536,2048]{1,0:T(8,128)(2,1)S(1)}, f32[1536,2048]{1,0:T(8,128)}, f32[1536,2048]{1,0:T(8,128)}) fusion(f32[2048]{0:T(1024)S(1)} %bitcast.334, bf16[2048,2048]{1,0:T(8,128)(2,1)} %all-gather.10.cloned.1.call-done, bf16[1536,2048]{1,0:T(8,128)(2,1)} %param.21, f32[2048]{0:T(1024)S(1)} %bitcast.330, f32[2048]{0:T(1024)S(1)} %bitcast.308, ...), kind=kOutput, calls=%fused_computation.70 | convolution fusion | flops 13111394304 | bytes 46174208 | tf_op jit(solution)/shard_map/dot_general | solution.py:196
  227.4 19.6 %fusion.94 = f32[2048,2048]{1,0:T(8,128)} fusion(bf16[1536,2048]{1,0:T(8,128)(2,1)S(1)} %get-tuple-element.368, f32[1536]{0:T(1024)S(1)} %reshape.412, bf16[1536,2048]{1,0:T(8,128)(2,1)} %param.22), kind=kOutput, calls=%fused_computation.224 | convolution fusion | flops 12894339072 | bytes 29366272 | tf_op jit(solution)/shard_map/dot_general | solution.py:80
  251.1 112.8 %reduce-scatter.27.cloned.1.call-done = f32[2048,256]{1,0:T(8,128)} async-done(((f32[2048,2048]{1,0:T(8,128)}), f32[2048,256]{1,0:T(8,128)}) %reduce-scatter.27.cloned.1.call-update) | async-done | bytes 2097168 | tf_op jit(solution)/shard_map/reduce_scatter | solution.py:260
  405.9 33.5 %while.27 = (s32[]{:T(128)}, f32[3,512,2,256]{1,3,2,0:T(8,128)}, f32[3,512,2,256]{1,3,2,0:T(8,128)}, bf16[3,512,2,256]{1,3,2,0:T(8,128)(2,1)}, bf16[3,512,2,256]...) while((s32[]{:T(128)}, f32[3,512,2,256]{1,3,2,0:T(8,128)}, ...), condition=%wide.region_9.10_spmd, body=%wide.region_7.9_spmd.sunk | while | flops 1347943936 | bytes 36724960 | solution.py:226
  458.7 13.0 %convert_element_type.139 = bf16[1536,1536]{1,0:T(8,128)(2,1)} reshape(bf16[3,512,2,3,256]{4,3,2,1,0:T(4,128)(2,1)} %copy.171) | data formatting | bytes 9437184 | tf_op jit(solution)/shard_map/convert_element_type | solution.py:234
  471.7 26.9 %convert_reduce_fusion = (f32[2048]{0:T(1024)S(1)}, bf16[1536,2048]{1,0:T(8,128)(2,1)}) fusion(f32[1536,2048]{1,0:T(8,128)} %get-tuple-element.369, bf16[2048,2048]{1,0:T(8,128)(2,1)} %all-gather.12.cloned.1.call-done, f32[1536]{0:T(1024)S(1)} %reshape.412, bf16[1536,2048]{1,0:T(8,128)(2,1)} %param.22, f32[1536,2048]{1,0:T(8,128)} %get-tuple-element.429, ...), kind=kOutput, calls=%fused_computation.63 | convolution fusion | flops 12947814400 | bytes 46159872 | tf_op jit(solution)/shard_map/dot_general | solution.py:86
  498.6 19.2 %fusion.110 = f32[1536,2048]{1,0:T(8,128)} fusion(bf16[1536,2048]{1,0:T(8,128)(2,1)} %get-tuple-element.432, bf16[2048,2048]{1,0:T(8,128)(2,1)} %all-gather.10.cloned.1.call-done), kind=kOutput, calls=%fused_computation.233 | convolution fusion | flops 12884901888 | bytes 27262976 | tf_op jit(solution)/shard_map/dot_general | solution.py:86
  517.8 22.2 %fusion.104 = (f32[2048]{0:T(1024)S(1)}, f32[1536]{0:T(1024)S(1)}, f32[1536]{0:T(1024)S(1)}, f32[2048]{0:T(1024)S(1)}, f32[1536,2048]{1,0:T(8,128)}) fusion(f32[2048]{0:T(1024)S(1)} %bitcast.314, f32[1536]{0:T(1024)S(1)} %copy-done.24, bf16[1536,2048]{1,0:T(8,128)(2,1)} %param.21, f32[1536,2048]{1,0:T(8,128)} %fusion.110, f32[2048]{0:T(1024)S(1)} %bitcast.309, ...), kind=kOutput, calls=%fused_computation.228 | convolution fusion | flops 9695125504 | bytes 42518528 | tf_op jit(solution)/shard_map/dot_general | solution.py:86
  540.1 14.1 %multiply_reduce_fusion.1 = (f32[2048]{0:T(1024)S(1)}, f32[1536]{0:T(1024)S(1)}, f32[1536]{0:T(1024)S(1)}, f32[2048]{0:T(1024)S(1)}) fusion(f32[1536,2048]{1,0:T(8,128)} %fusion.110, bf16[1536,2048]{1,0:T(8,128)(2,1)} %param.21, f32[1536]{0:T(1024)S(1)} %copy-done.32, f32[1536]{0:T(1024)S(1)} %copy-done.24, f32[1536]{0:T(1024)S(1)} %get-tuple-element.413, ...), kind=kLoop, calls=%fused_computation.61 | loop fusion | flops 59761664 | bytes 31526912 | tf_op jit(solution)/shard_map/transpose(jvp())/reduce_sum | solution.py:44
  556.2 16.7 %fusion.91 = f32[2048,1536]{1,0:T(8,128)} fusion(bf16[1536,1536]{1,0:T(8,128)(2,1)} %convert_element_type.139, bf16[1536,2048]{1,0:T(8,128)(2,1)} %param.21, f32[2048]{0:T(1024)S(1)} %bitcast.333, f32[2048]{0:T(1024)S(1)} %bitcast.316, f32[1536]{0:T(1024)S(1)} %copy-done.32, f32[1536]{0:T(1024)S(1)} %copy-done.24), kind=kOutput, calls=%fused_computation.221 | convolution fusion | flops 9682550784 | bytes 23621632 | tf_op jit(solution)/shard_map/dot_general | solution.py:80
  574.1 14.5 %reduce-scatter.29.cloned.1.call-done = f32[6,256]{1,0:T(8,128)} async-done(((f32[6,2048]{1,0:T(8,128)}), f32[6,256]{1,0:T(8,128)}) %reduce-scatter.29.cloned.1.call-update) | async-done | bytes 6160 | tf_op jit(solution)/shard_map/reduce_scatter | solution.py:257
  590.2 16.2 %add_convert_fusion = bf16[1536,2048]{1,0:T(8,128)(2,1)} fusion(f32[1536]{0:T(1024)S(1)} %negate_multiply_fusion.1, f32[1536]{0:T(1024)S(1)} %negate_multiply_fusion.2, f32[1536]{0:T(1024)S(1)} %get-tuple-element.412, f32[1536]{0:T(1024)S(1)} %copy-done.24, bf16[1536,2048]{1,0:T(8,128)(2,1)} %param.21, f32[1536]{0:T(1024)S(1)} %copy-done.32, ...), kind=kLoop, calls=%fused_computation.64 | loop fusion | flops 50331648 | bytes 37801984 | tf_op jit(solution)/shard_map/convert_element_type | solution.py:264
  615.6 21.3 %add_convert_fusion.2 = bf16[1536,2048]{1,0:T(8,128)(2,1)} fusion(f32[1536,2048]{1,0:T(8,128)} %fusion.109, bf16[1536,2048]{1,0:T(8,128)(2,1)} %copy-done.52, bf16[2048,2048]{1,0:T(8,128)(2,1)} %all-gather.12.cloned.1.call-done), kind=kOutput, calls=%fused_computation.69 | convolution fusion | flops 12891193344 | bytes 33554432 | tf_op jit(solution)/shard_map/dot_general | solution.py:201
  637.5 24.6 %fusion.89 = f32[2048,2048]{1,0:T(8,128)} fusion(bf16[1536,2048]{1,0:T(8,128)(2,1)} %get-tuple-element.432, bf16[1536,2048]{1,0:T(8,128)(2,1)} %param.21, f32[2048]{0:T(1024)S(1)} %bitcast.331, f32[2048]{0:T(1024)S(1)} %bitcast.312, f32[1536]{0:T(1024)S(1)} %copy-done.32, f32[1536]{0:T(1024)S(1)} %copy-done.24), kind=kOutput, calls=%fused_computation.219 | convolution fusion | flops 12903776256 | bytes 29388800 | tf_op jit(solution)/shard_map/dot_general | solution.py:80
  675.3 47.3 %reduce-scatter.21.cloned.1.call-done = f32[256,1536]{1,0:T(8,128)} async-done(((f32[2048,1536]{1,0:T(8,128)}), f32[256,1536]{1,0:T(8,128)}) %reduce-scatter.21.cloned.1.call-update) | async-done | bytes 1572880 | tf_op jit(solution)/shard_map/reduce_scatter | solution.py:254
  732.9 27.3 %reduce-scatter.33.cloned.1.call-done = f32[128,2]{1,0:T(8,128)} async-done(((f32[1024,2]{1,0:T(8,128)}), f32[128,2]{1,0:T(8,128)}) %reduce-scatter.33.cloned.1.call-update) | async-done | bytes 1040
  763.2 19.2 %reduce-scatter.35.cloned.1.call-done = bf16[64,4]{1,0:T(8,128)(2,1)} async-done(((bf16[256,4]{1,0:T(8,128)(2,1)}), bf16[64,4]{1,0:T(8,128)(2,1)}) %reduce-scatter.35.cloned.1.call-update) | async-done | bytes 528
  784.5 109.1 %reduce-scatter.19.cloned.1.call-done = bf16[1536,512]{1,0:T(8,128)(2,1)} async-done(((bf16[1536,2048]{1,0:T(8,128)(2,1)}), bf16[1536,512]{1,0:T(8,128)(2,1)}) %reduce-scatter.19.cloned.1.call-update) | async-done | bytes 1572880 | tf_op jit(solution)/shard_map/reduce_scatter | solution.py:263
  897.6 109.6 %reduce-scatter.17.cloned.1.call-done = bf16[1536,512]{1,0:T(8,128)(2,1)} async-done(((bf16[1536,2048]{1,0:T(8,128)(2,1)}), bf16[1536,512]{1,0:T(8,128)(2,1)}) %reduce-scatter.17.cloned.1.call-update) | async-done | bytes 1572880 | tf_op jit(solution)/shard_map/reduce_scatter | solution.py:204
  1011.2 116.7 %reduce-scatter.25.cloned.1.call-done = f32[256,2048]{1,0:T(8,128)} async-done(((f32[2048,2048]{1,0:T(8,128)}), f32[256,2048]{1,0:T(8,128)}) %reduce-scatter.25.cloned.1.call-update) | async-done | bytes 2097168 | tf_op jit(solution)/shard_map/reduce_scatter | solution.py:258
  (312 shorter events, 281.0 us)
Async XLA Ops:
  7.2 51.8 %all-gather.6.cloned.1.call-start = ((), (), s32[]{:S(2)}) async-start(), calls=%async_computation.10 | async-start | bytes 7077888 | tf_op jit(solution)/shard_map/all_gather | solution.py:170
  9.6 167.3 %all-gather.10.cloned.1.call-start = ((), (), s32[]{:S(2)}) async-start(), calls=%async_computation.12 | async-start | bytes 9437184 | tf_op jit(solution)/shard_map/all_gather | solution.py:173
  10.4 14.4 %collective-permute-start = (bf16[6,64]{1,0:T(8,128)(2,1)S(1)}, bf16[6,64]{1,0:T(8,128)(2,1)S(1)}, u32[]{:S(2)}, u32[]{:S(2)}) collective-permute-start(bf16[6,64]{1,0:T(8,128)(2,1)S(1)} %convert_element_type.120), channel_id=1, source_target_pairs={{0,1},{1,0},{2,3},{3,2},{4,5},{5,4},{6,7},{7,6},{8,9},{9,8},{10,11... | collective-permute-start | bytes 2312 | tf_op jit(solution)/shard_map/ppermute | solution.py:29
  16.2 230.9 %reduce-scatter.23.cloned.1.call-start = ((), (), s32[]{:S(2)}) async-start(), calls=%async_computation.17 | async-start | bytes 4718592 | tf_op jit(solution)/shard_map/reduce_scatter | solution.py:256
  21.2 155.7 %copy-start.23 = (f32[1536]{0:T(1024)}, f32[1536]{0:T(1024)S(1)}, u32[]{:S(2)}) copy-start(f32[1536]{0:T(1024)S(1)} %broadcast_multiply_fusion) | copy-start | bytes 18436
  24.8 11.4 collective-permute-start.1
  36.2 10.0 collective-permute-start.2
  46.2 4.0 collective-permute-start.3
  50.3 4.3 collective-permute-start.4
  51.1 420.6 %copy-start.29 = (f32[1536]{0:T(1024)}, f32[1536]{0:T(1024)S(1)}, u32[]{:S(2)}) copy-start(f32[1536]{0:T(1024)S(1)} %reshape.412) | copy-start | bytes 18436
  176.8 187.1 %reduce-scatter.27.cloned.1.call-start = ((), (), s32[]{:S(2)}) async-start(), calls=%async_computation.19 | async-start | bytes 18874368 | tf_op jit(solution)/shard_map/reduce_scatter | solution.py:260
  247.0 146.8 %all-gather.8.cloned.1.call-start = ((), (), s32[]{:S(2)}) async-start(), calls=%async_computation.11 | async-start | bytes 2359296 | tf_op jit(solution)/shard_map/all_gather | solution.py:172
  251.1 220.7 %all-gather.12.cloned.1.call-start = ((), (), s32[]{:S(2)}) async-start(), calls=%async_computation.13 | async-start | bytes 9437184 | tf_op jit(solution)/shard_map/all_gather | solution.py:175
  370.8 217.8 %reduce-scatter.29.cloned.1.call-start = ((), (), s32[]{:S(2)}) async-start(), calls=%async_computation.20 | async-start | bytes 73728 | tf_op jit(solution)/shard_map/reduce_scatter | solution.py:257
  555.0 118.2 %reduce-scatter.31.cloned.1.call-start = ((), (), s32[]{:S(2)}) async-start(), calls=%async_computation.21 | async-start | bytes 442368
  556.2 166.4 %reduce-scatter.21.cloned.1.call-start = ((), (), s32[]{:S(2)}) async-start(), calls=%async_computation.16 | async-start | bytes 14155776 | tf_op jit(solution)/shard_map/reduce_scatter | solution.py:254
  572.9 187.3 %reduce-scatter.33.cloned.1.call-start = ((), (), s32[]{:S(2)}) async-start(), calls=%async_computation.22 | async-start | bytes 589824
  574.1 208.3 %reduce-scatter.35.cloned.1.call-start = ((), (), s32[]{:S(2)}) async-start(), calls=%async_computation.23 | async-start | bytes 81920
  590.1 303.5 %reduce-scatter.19.cloned.1.call-start = ((), (), s32[]{:S(2)}) async-start(), calls=%async_computation.15 | async-start | bytes 7864320 | tf_op jit(solution)/shard_map/reduce_scatter | solution.py:263
  606.4 400.8 %reduce-scatter.17.cloned.1.call-start = ((), (), s32[]{:S(2)}) async-start(), calls=%async_computation.14 | async-start | bytes 7864320 | tf_op jit(solution)/shard_map/reduce_scatter | solution.py:204
  636.9 491.1 %reduce-scatter.25.cloned.1.call-start = ((), (), s32[]{:S(2)}) async-start(), calls=%async_computation.18 | async-start | bytes 18874368 | tf_op jit(solution)/shard_map/reduce_scatter | solution.py:258
  732.9 274.3 %copy-start.30 = (f32[1536]{0:T(1024)S(1)}, f32[1536]{0:T(1024)}, u32[]{:S(2)}) copy-start(f32[1536]{0:T(1024)} %copy-done.29) | copy-start | bytes 18436
  761.2 250.0 %copy-start.42 = (f32[2,128]{1,0:T(2,128)}, f32[2,128]{1,0:T(2,128)S(1)}, u32[]{:S(2)}) copy-start(f32[2,128]{1,0:T(2,128)S(1)} %copy.186) | copy-start | bytes 3076
  897.6 230.3 %copy-start.6 = (f32[256,2048]{1,0:T(8,128)S(1)}, f32[256,2048]{1,0:T(8,128)}, u32[]{:S(2)}) copy-start(f32[256,2048]{1,0:T(8,128)} %param.30) | copy-start | bytes 6291460
  (52 other events, 1547.3 us)
Sparse Core Ops, SparseCore 0:
  10.5 48.4 all-gather.5
  61.4 54.2 all-gather.9
  176.9 51.7 reduce-scatter.22
  247.1 116.7 reduce-scatter.26
  365.6 28.1 all-gather.7
  396.1 55.8 all-gather.11
  555.1 33.5 reduce-scatter.28
  592.3 33.8 reduce-scatter.30
  630.3 92.2 reduce-scatter.20
  726.1 34.1 reduce-scatter.32
  763.1 19.2 reduce-scatter.34
  784.6 108.9 reduce-scatter.18
  895.9 111.2 reduce-scatter.16
  1011.2 116.6 reduce-scatter.24
